TPU v7x, 32 devices: a whole 2x2x4 slice. The times are simulated.
32 devices in a mesh: pb: 4 (over x, core), dev: 8 (over z, y).
Axes of the slice: x: 2, y: 2, z: 4, core: 2. Of those that a mesh axis runs over, the one named last changes fastest.
Arguments:
- queries: bfloat16 [64, 768], P(('pb', 'dev')), may hold values from -6 to 6
- probes: int32 [64, 16], P(('pb', 'dev')), may hold values from 0 to 1023, all different within a row
- vectors: bfloat16 [16384, 768], P(('pb', 'dev')), may hold values from -0.4375 to 0.4375
- list_ids: int32 [16384], P(('pb', 'dev')), may hold values from 0 to 1023, as said below
Outputs:
- leaders: float32 [64, 100], P(('pb', 'dev'))
Inputs may be any that keep to these rules, and one draw needn't show every extreme that they name: `list_ids`: each list id names exactly 16 database vectors. `probes`: each query names 16 different lists.
All inputs are finite; a program needn't handle non-finite values.
Results may differ from a plain program's by a relative error of at most 0.0004.
Values may be sent and summed in bfloat16 or wider, within the bound.
A program may use at most 64 MiB of HBM per device.

v0:
```python
import math

import jax
import jax.numpy as jnp
from jax import lax
from jax.sharding import PartitionSpec as P

K = 100
NLIST = 1024


masked_value = -1e30


def filtered_scores(block_rows, block_probes, slab_part, list_onehot):
    products = lax.dot_general(
        block_rows, slab_part, (((1,), (1,)), ((), ())), preferred_element_type=jnp.float32
    )
    count = block_rows.shape[0]
    row_index = lax.broadcasted_iota(jnp.int32, block_probes.shape, 0)
    hits = (
        jnp.zeros((count, list_onehot.shape[0]), jnp.bfloat16)
        .at[row_index, block_probes]
        .set(jnp.bfloat16(1.0))
    )
    matches = jnp.dot(hits, list_onehot, preferred_element_type=jnp.float32)
    return jnp.where(matches > 0.5, products, jnp.float32(masked_value))


def local(queries, probes, vectors, list_ids):
    local_count = min(K, vectors.shape[0])
    list_index = lax.broadcasted_iota(jnp.int32, (NLIST, list_ids.shape[0]), 0)
    list_onehot = (list_index == list_ids[None, :]).astype(jnp.bfloat16)
    block_rows, block_probes = lax.all_gather((queries, probes), ("pb", "dev"), axis=0, tiled=True)
    count = block_rows.shape[0]
    width = math.gcd(count, 256)

    def one_block(block_args):
        rows_here, probes_here = block_args
        kept, _ = lax.top_k(
            filtered_scores(rows_here, probes_here, vectors, list_onehot), local_count
        )
        return kept

    kept = lax.map(
        one_block,
        (
            block_rows.reshape(count // width, width, block_rows.shape[1]),
            block_probes.reshape(count // width, width, block_probes.shape[1]),
        ),
    )
    candidates = kept.reshape(count, local_count)
    pooled = lax.all_to_all(
        lax.all_to_all(candidates, "pb", split_axis=0, concat_axis=1, tiled=True),
        "dev",
        split_axis=0,
        concat_axis=1,
        tiled=True,
    )
    leaders, _ = lax.top_k(pooled, K)
    return leaders


def solution(mesh):
    return jax.shard_map(
        local,
        mesh=mesh,
        in_specs=(
            P(("pb", "dev"), None),
            P(("pb", "dev"), None),
            P(("pb", "dev"), None),
            P(("pb", "dev")),
        ),
        out_specs=P(("pb", "dev"), None),
        check_vma=False,
    )
```

profile of v0, /device:TPU:0, one launch (start us, length us, event | category | flops | bytes accessed | tf_op | source)
XLA Modules:
  0.0 173.4 jit_solution(18283265919945762596)
XLA Ops:
  0.0 0.0 copy-start
  0.0 0.0 copy-start.1
  0.0 70.2 %all-gather = s32[32,2,16]{2,1,0:T(2,128)S(1)} all-gather(s32[1,2,16]{2,1,0:T(2,128)} %bitcast.16), channel_id=1, replica_groups=mesh['pb'=4,'dev'=8] {'pb','dev'}, dimensions={0}, use_global_device_ids=true | all-gather | bytes 4224 | tf_op jit(solution)/shard_map/all_gather | solution.py:34
  70.2 0.1 copy.13
  70.3 0.7 multiply_reduce_fusion
  71.0 0.7 and_reduce_fusion
  71.8 0.1 copy.16
  71.9 0.1 reshape.32
  71.9 7.7 %scatter_custom_fusion = bf16[65536]{0:T(1024)(128)(2,1)S(1)} fusion(s32[1024]{0:T(1024)S(1)} %reshape.32, bf16[1024]{0:T(1024)(128)(2,1)S(1)} %broadcast.64, bf16[]{:T(256)} %constant.41.clone.1), kind=kCustom, calls=%fused_computation.6 | custom fusion | bytes 131074
  79.6 0.1 reshape.31
  79.7 64.1 %all-gather.1 = bf16[32,2,768]{2,1,0:T(2,128)(2,1)S(1)} all-gather(bf16[1,2,768]{2,1,0:T(2,128)(2,1)} %bitcast.15), channel_id=1, replica_groups=mesh['pb'=4,'dev'=8] {'pb','dev'}, dimensions={0}, use_global_device_ids=true | all-gather | bytes 101376 | tf_op jit(solution)/shard_map/all_gather | solution.py:34
  143.8 0.0 copy-done.1
  143.8 0.5 fusion.1
  144.3 0.0 copy-done
  144.3 0.4 convolution_select_fusion
  144.7 3.2 %sort_prefixfusion = f32[64,100]{1,0:T(8,128)S(1)} fusion(f32[64,512]{1,0:T(8,128)S(1)} %convolution_select_fusion), kind=kCustom, calls=%top_k.14.sort_prefix | custom fusion | flops 491520 | bytes 156672 | tf_op jit(solution)/shard_map/while/body/eval_jaxpr/top_k | solution.py:40
  147.9 6.3 %all_to_all.35 = f32[4,16,100]{2,1,0:T(8,128)S(1)} all-to-all(f32[4,16,100]{2,1,0:T(8,128)S(1)} %bitcast.11), channel_id=1, replica_groups=mesh['pb'=4,'dev'=8] {'pb'}, dimensions={0} | all-to-all | bytes 51200 | tf_op jit(solution)/shard_map/all_to_all | solution.py:54
  154.2 0.1 all_to_all.29
  154.3 10.0 %all_to_all.36 = f32[8,2,400]{2,1,0:T(2,128)S(1)} all-to-all(f32[8,2,400]{2,1,0:T(2,128)S(1)} %all_to_all.29), channel_id=1, replica_groups=mesh['pb'=4,'dev'=8] {'dev'}, dimensions={0} | all-to-all | bytes 51200 | tf_op jit(solution)/shard_map/all_to_all | solution.py:53
  164.3 0.1 all_to_all.32
  164.4 8.4 %top_k.20 = (f32[2,3200]{1,0:T(2,128)S(1)}, s32[2,3200]{1,0:T(2,128)}) sort(f32[2,3200]{1,0:T(2,128)S(1)} %all_to_all.32, s32[2,3200]{1,0:T(2,128)S(1)} %iota.24), dimensions={1}, to_apply=%region_2.3 | sort | flops 83200 | bytes 102400 | tf_op jit(solution)/shard_map/top_k | solution.py:60
  172.8 0.6 top_k.21
  (8 shorter events, 0.1 us)
Async XLA Ops:
  0.0 144.3 %copy-start = (bf16[512,768]{1,0:T(8,128)(2,1)S(1)}, bf16[512,768]{1,0:T(8,128)(2,1)}, u32[]{:S(2)}) copy-start(bf16[512,768]{1,0:T(8,128)(2,1)} %param.6) | copy-start | bytes 2359300
  0.0 143.8 %copy-start.1 = (s32[512]{0:T(512)S(1)}, s32[512]{0:T(512)}, u32[]{:S(2)}) copy-start(s32[512]{0:T(512)} %param.7) | copy-start | bytes 6148
where the time goes:
time: 174 us; the launch traced here: 173 us
  blocking collectives  151 us (87%)
  other arithmetic  13.1 us (8%)
  local copies, waits for them, and re-layouts  8.8 us (5%)
    all_gather x2, blocking collectives, local(): lax.all_gather((queries, probes), ('pb', 'dev'), axis=0, tiled=True)  134 us
    all_to_all x1, blocking collectives, local(): lax.all_to_all(lax.all_to_all(candidates, 'pb', split_axis=0, concat_axis...  9.97 us
    top_k x1, other arithmetic, local(): leaders, _ = lax.top_k(pooled, K)  8.39 us
    unnamed x10, local copies, waits for them, and re-layouts  7.93 us
    all_to_all x1, blocking collectives, local(): lax.all_to_all(candidates, 'pb', split_axis=0, concat_axis=1, tiled=True)  6.3 us

commit v1 on v0

v1 whole, which is shorter than its diff:
```python
import functools

import jax
import jax.numpy as jnp
from jax import lax
from jax.experimental import pallas as pl
from jax.experimental.pallas import tpu as pltpu
from jax.sharding import PartitionSpec as P

K = 100
LIST = 128
SUB = 8
REGS = LIST // SUB
masked_value = -1e30
MESH = pl.DeviceIdType.MESH


def sublane_index():
    return lax.broadcasted_iota(jnp.int32, (SUB, LIST), 0)


def lane_index():
    return lax.broadcasted_iota(jnp.int32, (SUB, LIST), 1)


def sign_where(condition):
    return jnp.where(condition, jnp.float32(-1.0), jnp.float32(1.0))


def register_stage(regs, distance, size):
    out = list(regs)
    for v in range(REGS):
        if v & distance:
            continue
        high, low = jnp.maximum(regs[v], regs[v | distance]), jnp.minimum(regs[v], regs[v | distance])
        if v & size:
            high, low = low, high
        out[v], out[v | distance] = high, low
    return out


def sublane_stage(regs, distance, sub):
    upper = (sub & distance) != 0
    out = []
    for x in regs:
        if 2 * distance == SUB:
            partner = pltpu.roll(x, distance, 0)
        else:
            partner = jnp.where(upper, pltpu.roll(x, distance, 0), pltpu.roll(x, SUB - distance, 0))
        out.append(jnp.where(upper, jnp.minimum(x, partner), jnp.maximum(x, partner)))
    return out


def resort(regs, sub):
    for distance in (4, 2, 1):
        regs = sublane_stage(regs, distance, sub)
    for distance in (8, 4, 2, 1):
        regs = register_stage(regs, distance, 0)
    return regs


def times(regs, sign):
    return [x * sign for x in regs]


def sort_list(regs, sub, sign):
    for size in (2, 4, 8):
        distance = size // 2
        while distance:
            regs = register_stage(regs, distance, size)
            distance //= 2
    now = sign_where((sub & 1) != 0)
    regs = times(regs, now)
    for distance in (8, 4, 2, 1):
        regs = register_stage(regs, distance, 0)
    for step in (1, 2):
        following = sign_where((sub & (2 * step)) != 0)
        regs = times(regs, now * following)
        now = following
        distance = step
        while distance:
            regs = sublane_stage(regs, distance, sub)
            distance //= 2
        for distance in (8, 4, 2, 1):
            regs = register_stage(regs, distance, 0)
    regs = times(regs, now * sign)
    return times(resort(regs, sub), sign)


def split(block):
    return [block[SUB * v : SUB * (v + 1)] for v in range(REGS)]


def join(regs):
    return jnp.concatenate(regs, axis=0)


def larger(left, right):
    return [jnp.maximum(x, y) for x, y in zip(left, right)]


def local_lists(scores, sign):
    sub, lane = sublane_index(), lane_index()
    lists = [split(scores[LIST * i : LIST * (i + 1)]) for i in range(scores.shape[0] // LIST)]
    one, other = jnp.ones((SUB, LIST), jnp.float32), jnp.full((SUB, LIST), -1.0, jnp.float32)
    half_sign = sign_where(lane >= LIST // 2)
    if len(lists) == 1:
        kept = sort_list(lists[0], sub, half_sign)
    else:
        kept = sort_list(lists[0], sub, one)
        for i, item in enumerate(lists[1:]):
            kept = larger(kept, sort_list(item, sub, other))
            final = half_sign if i == len(lists) - 2 else one
            kept = times(resort(times(kept, final), sub), final)
    kept = larger(kept, [pltpu.roll(x, LIST // 2, 1) for x in kept])
    return times(resort(times(kept, sign), sub), sign)


def merge_all(rows, per_device):
    sub, lane = sublane_index(), lane_index()
    pieces = [rows[i : i + LIST] for i in range(0, rows.shape[0], LIST)]
    lanes = pieces[0].shape[0]
    if lanes < LIST:
        pieces = [jnp.concatenate([pieces[0]] * (LIST // lanes), axis=0)]
    blocks = [split(piece.T) for piece in pieces]
    while len(blocks) > 1:
        half = len(blocks) // 2
        merged = [larger(blocks[i], blocks[i + half]) for i in range(half)]
        blocks = []
        for i, regs in enumerate(merged):
            if half == 1:
                sign = sign_where((lane & (lanes // 2)) != 0)
            else:
                sign = jnp.full((SUB, LIST), -1.0 if i >= half // 2 else 1.0, jnp.float32)
            blocks.append(times(resort(times(regs, sign), sub), sign))
    regs = blocks[0]
    stride = lanes // 2
    while stride >= per_device:
        regs = larger(regs, [pltpu.roll(x, LIST - stride, 1) for x in regs])
        stride //= 2
        if stride >= per_device:
            sign = sign_where((lane & stride) != 0)
            regs = times(resort(times(regs, sign), sub), sign)
        else:
            regs = resort(regs, sub)
    return regs


def kernel(
    axes, q_ref, p_ref, v_hbm, id_ref, out_ref,
    v_ref, all_q, all_p, best, arrived, v_sem, own_sem, q_sems, p_sems, s_sems,
):
    (outer, n_outer), (inner, n_inner) = axes
    n = n_outer * n_inner
    me = lax.axis_index(outer) * n_inner + lax.axis_index(inner)
    per_device, depth = q_ref.shape
    rows = v_ref.shape[0]

    def device(k):
        other = lax.rem(me + k, n)
        return other, (other // n_inner, lax.rem(other, n_inner))

    load = pltpu.make_async_copy(v_hbm, v_ref, v_sem)
    load.start()
    own = [
        pltpu.make_async_copy(q_ref, all_q.at[me], own_sem.at[0]),
        pltpu.make_async_copy(p_ref, all_p.at[me], own_sem.at[1]),
    ]
    for copy in own:
        copy.start()

    barrier = pltpu.get_barrier_semaphore()

    @pl.loop(1, n)
    def _(k):
        pl.semaphore_signal(barrier, inc=1, device_id=device(k)[1], device_id_type=MESH)

    pl.semaphore_wait(barrier, n - 1)

    def query_copies(k):
        target = device(k)[1]
        return [
            pltpu.make_async_remote_copy(
                src_ref=src, dst_ref=dst.at[me], send_sem=sems.at[0, k], recv_sem=sems.at[1, k],
                device_id=target, device_id_type=MESH,
            )
            for src, dst, sems in ((q_ref, all_q, q_sems), (p_ref, all_p, p_sems))
        ]

    def score_copy(k):
        other, target = device(k)
        return pltpu.make_async_remote_copy(
            src_ref=best.at[other], dst_ref=arrived.at[me], send_sem=s_sems.at[0, k], recv_sem=s_sems.at[1, k],
            device_id=target, device_id_type=MESH,
        )

    @pl.loop(1, n)
    def _(k):
        for copy in query_copies(k):
            copy.start()

    for copy in own:
        copy.wait()
    load.wait()

    @pl.loop(1, n)
    def _(k):
        for copy in query_copies(k):
            copy.wait()

    lane = lane_index()
    sign = jnp.where(me >= n // 2, jnp.float32(-1.0), jnp.float32(1.0))
    half = LIST // 2
    span = half // per_device
    low_lanes = lax.broadcasted_iota(jnp.int32, (rows // 2, LIST), 1) < half
    ids = jnp.where(
        low_lanes,
        jnp.broadcast_to(id_ref[: rows // 2], (rows // 2, LIST)),
        jnp.broadcast_to(id_ref[rows // 2 :], (rows // 2, LIST)),
    )

    def one_block(b):
        here = pl.ds(b * span, span)
        queries = all_q[here].astype(jnp.float32).reshape(half, depth).astype(jnp.bfloat16)
        queries = jnp.concatenate([queries, queries], axis=0)
        probes = all_p[here].reshape(half, all_p.shape[-1])
        probes = jnp.concatenate([probes, jnp.zeros((half, LIST - probes.shape[1]), jnp.int32)], axis=1)
        probes = jnp.concatenate([probes, probes], axis=0).T
        products = lax.dot_general(
            v_ref[...], queries, (((1,), (1,)), ((), ())), preferred_element_type=jnp.float32
        )
        products = jnp.where(low_lanes, products[: rows // 2], products[rows // 2 :])
        hit = ids == probes[0:1]
        for p in range(1, all_p.shape[-1]):
            hit = hit | (ids == probes[p : p + 1])
        scores = jnp.where(hit, products, jnp.float32(masked_value))
        kept = join(local_lists(scores, sign))
        best[here] = kept.T[:half].reshape(span, per_device, LIST)

    if n == span:
        one_block(0)
    else:
        pl.loop(0, n // span)(one_block)

    @pl.loop(1, n)
    def _(k):
        score_copy(k).start()

    keep = pltpu.make_async_copy(best.at[me], arrived.at[me], own_sem.at[0])
    keep.start()
    keep.wait()

    @pl.loop(1, n)
    def _(k):
        score_copy(k).wait()

    regs = merge_all(arrived[...].reshape(n * per_device, LIST), per_device)
    table = join(regs).reshape(REGS, SUB, LIST)
    ordered = jnp.concatenate([table[:, s] for s in range(SUB)], axis=0)
    out_ref[...] = ordered.T[:per_device, :K]


def solution(mesh):
    axes = tuple(mesh.shape.items())
    n = mesh.size

    def local(queries, probes, vectors, list_ids):
        per_device, depth = queries.shape
        rows = vectors.shape[0]
        return pl.pallas_call(
            functools.partial(kernel, axes),
            out_shape=jax.ShapeDtypeStruct((per_device, K), jnp.float32),
            in_specs=[
                pl.BlockSpec(memory_space=pltpu.VMEM),
                pl.BlockSpec(memory_space=pltpu.VMEM),
                pl.BlockSpec(memory_space=pl.ANY),
                pl.BlockSpec(memory_space=pltpu.VMEM),
            ],
            out_specs=pl.BlockSpec(memory_space=pltpu.VMEM),
            scratch_shapes=[
                pltpu.VMEM((rows, depth), vectors.dtype),
                pltpu.VMEM((n, per_device, depth), queries.dtype),
                pltpu.VMEM((n, per_device, probes.shape[1]), probes.dtype),
                pltpu.VMEM((n, per_device, LIST), jnp.float32),
                pltpu.VMEM((n, per_device, LIST), jnp.float32),
                pltpu.SemaphoreType.DMA,
                pltpu.SemaphoreType.DMA((2,)),
                pltpu.SemaphoreType.DMA((2, n)),
                pltpu.SemaphoreType.DMA((2, n)),
                pltpu.SemaphoreType.DMA((2, n)),
            ],
            compiler_params=pltpu.CompilerParams(collective_id=0, has_side_effects=True),
        )(queries, probes, vectors, list_ids[:, None])

    return jax.shard_map(
        local,
        mesh=mesh,
        in_specs=(
            P(("pb", "dev"), None),
            P(("pb", "dev"), None),
            P(("pb", "dev"), None),
            P(("pb", "dev")),
        ),
        out_specs=P(("pb", "dev"), None),
        check_vma=False,
    )
```

time: 174 us -> 25.4 us (0.15)
  blocking collectives: 151 us -> 0 us
  Pallas kernels: 0 us -> 22.4 us
  other arithmetic: 13.1 us -> 0 us
  local copies, waits for them, and re-layouts: 8.8 us -> 2.75 us
    all_gather x2 -> x0, blocking collectives: 134 us -> none  [local(): lax.all_gather((queries, probes), ('pb', 'dev'), axis=0, tiled=True)]
    pallas_call x0 -> x1, Pallas kernels: none -> 22.4 us  [local(): pl.pallas_call(functools.partial(kernel, axes), out_shape=jax.ShapeDtypeS...]
    all_to_all x2 -> x0, blocking collectives: 16.3 us -> none  [the longest x1 9.97 us: local(): lax.all_to_all(lax.all_to_all(candidates, 'pb', split_axis=0, concat_axis...]
    top_k x2 -> x0, other arithmetic: 11.6 us -> none  [the longest x1 8.39 us: local(): leaders, _ = lax.top_k(pooled, K)]
    unnamed x10 -> x1, local copies, waits for them, and re-layouts: 7.93 us -> 1.23 us
where the time goes in v1:
time: 25.4 us; the launch traced here: 25.2 us
  Pallas kernels  22.4 us (88%)
  local copies, waits for them, and re-layouts  2.75 us (11%)
    pallas_call x1, Pallas kernels, local(): pl.pallas_call(functools.partial(kernel, axes), out_shape=jax.ShapeDtypeS...  22.4 us
    broadcast_in_dim x1, local copies, waits for them, and re-layouts, local(): list_ids[:, None]  1.52 us
    unnamed x1, local copies, waits for them, and re-layouts  1.23 us

profile of v1, /device:TPU:0, one launch (start us, length us, event | category | flops | bytes accessed | tf_op | source)
XLA Modules:
  0.0 25.2 jit_solution(14515252817135529384)
XLA Ops:
  0.0 1.5 %copy.5.id_ref = s32[512,1]{1,0:T(8,128)} copy(s32[512,1]{0,1:T(1,128)} %bitcast.1) | data formatting | bytes 4096 | tf_op jit(solution)/shard_map/broadcast_in_dim | solution.py:293
  1.5 22.4 %shard_map.46 = f32[2,100]{1,0:T(2,128)} custom-call(bf16[2,768]{1,0:T(2,128)(2,1)} %q_ref.1, s32[2,16]{1,0:T(2,128)} %p_ref.1, bf16[512,768]{1,0:T(8,128)(2,1)} %v_hbm.1, s32[512,1]{1,0:T(8,128)} %copy.5.id_ref), custom_call_target="tpu_custom_call" | custom-call | tf_op jit(solution)/shard_map/pallas_call | solution.py:270
  24.0 1.2 %copy.7 = f32[2,100]{1,0:T(2,128)} copy(f32[2,100]{1,0:T(2,128)} %shard_map.46) | data formatting | bytes 1600

commit v2 on v1

--- a/solution.py
+++ b/solution.py
@@ -147,77 +147,90 @@
 
 
 def kernel(
-    axes, q_ref, p_ref, v_hbm, id_ref, out_ref,
-    v_ref, all_q, all_p, best, arrived, v_sem, own_sem, q_sems, p_sems, s_sems,
+    axes, q_hbm, p_hbm, v_hbm, id_hbm, arrived,
+    q_ref, p_ref, v_ref, id_ref, all_q, all_p, best, load_sems, own_sems, q_sems, p_sems, s_sems,
 ):
     (outer, n_outer), (inner, n_inner) = axes
     n = n_outer * n_inner
-    me = lax.axis_index(outer) * n_inner + lax.axis_index(inner)
+    mine = lax.axis_index(outer), lax.axis_index(inner)
+    me = mine[0] * n_inner + mine[1]
     per_device, depth = q_ref.shape
     rows = v_ref.shape[0]
 
+    flips = [[(1 - 2 * ((at // 2**i) % 2)) * 2**i for i in range(n_axis.bit_length() - 1)] for at, n_axis in zip(mine, (n_outer, n_inner))]
+
+    def flipped(at, bits, k):
+        for i, flip in enumerate(bits):
+            if isinstance(k, int):
+                at = at + flip if (k >> i) & 1 else at
+            else:
+                at = at + flip * ((k // 2**i) % 2)
+        return at
+
     def device(k):
-        other = lax.rem(me + k, n)
-        return other, (other // n_inner, lax.rem(other, n_inner))
-
-    load = pltpu.make_async_copy(v_hbm, v_ref, v_sem)
-    load.start()
+        target = flipped(mine[0], flips[0], k // n_inner), flipped(mine[1], flips[1], k % n_inner)
+        return target[0] * n_inner + target[1], target
+
+    def for_peers(body):
+        if n <= 64:
+            for k in range(n - 1, 0, -1):
+                body(k)
+        else:
+            pl.loop(1, n)(body)
+
+    barrier = pltpu.get_barrier_semaphore()
+    for_peers(lambda k: pl.semaphore_signal(barrier, inc=1, device_id=device(k)[1], device_id_type=MESH))
+    loads = [
+        pltpu.make_async_copy(src, dst, load_sems.at[i])
+        for i, (src, dst) in enumerate(((q_hbm, q_ref), (p_hbm, p_ref), (id_hbm, id_ref), (v_hbm, v_ref)))
+    ]
+    for copy in loads:
+        copy.start()
     own = [
-        pltpu.make_async_copy(q_ref, all_q.at[me], own_sem.at[0]),
-        pltpu.make_async_copy(p_ref, all_p.at[me], own_sem.at[1]),
+        pltpu.make_async_copy(q_ref, all_q.at[me], own_sems.at[0]),
+        pltpu.make_async_copy(p_ref, all_p.at[me], own_sems.at[1]),
     ]
-    for copy in own:
+    for load, copy in zip(loads[:2], own):
+        load.wait()
         copy.start()
-
-    barrier = pltpu.get_barrier_semaphore()
-
-    @pl.loop(1, n)
-    def _(k):
-        pl.semaphore_signal(barrier, inc=1, device_id=device(k)[1], device_id_type=MESH)
-
     pl.semaphore_wait(barrier, n - 1)
+
+    def remote(src, dst, sems, k, target):
+        return pltpu.make_async_remote_copy(
+            src_ref=src, dst_ref=dst, send_sem=sems.at[0, k], recv_sem=sems.at[1, k],
+            device_id=target, device_id_type=MESH,
+        )
 
     def query_copies(k):
         target = device(k)[1]
-        return [
-            pltpu.make_async_remote_copy(
-                src_ref=src, dst_ref=dst.at[me], send_sem=sems.at[0, k], recv_sem=sems.at[1, k],
-                device_id=target, device_id_type=MESH,
-            )
-            for src, dst, sems in ((q_ref, all_q, q_sems), (p_ref, all_p, p_sems))
-        ]
+        return [remote(q_ref, all_q.at[me], q_sems, k, target), remote(p_ref, all_p.at[me], p_sems, k, target)]
 
     def score_copy(k):
         other, target = device(k)
-        return pltpu.make_async_remote_copy(
-            src_ref=best.at[other], dst_ref=arrived.at[me], send_sem=s_sems.at[0, k], recv_sem=s_sems.at[1, k],
-            device_id=target, device_id_type=MESH,
-        )
-
-    @pl.loop(1, n)
-    def _(k):
+        return remote(best.at[other], arrived.at[me], s_sems, k, target)
+
+    def start_queries(k):
         for copy in query_copies(k):
             copy.start()
 
-    for copy in own:
-        copy.wait()
-    load.wait()
-
-    @pl.loop(1, n)
-    def _(k):
+    def wait_queries(k):
         for copy in query_copies(k):
             copy.wait()
+
+    for_peers(start_queries)
+    for copy in own + loads[2:]:
+        copy.wait()
 
     lane = lane_index()
     sign = jnp.where(me >= n // 2, jnp.float32(-1.0), jnp.float32(1.0))
     half = LIST // 2
     span = half // per_device
     low_lanes = lax.broadcasted_iota(jnp.int32, (rows // 2, LIST), 1) < half
-    ids = jnp.where(
-        low_lanes,
-        jnp.broadcast_to(id_ref[: rows // 2], (rows // 2, LIST)),
-        jnp.broadcast_to(id_ref[rows // 2 :], (rows // 2, LIST)),
+    columns = jnp.concatenate(
+        [jnp.broadcast_to(id_ref[c : c + 1], (LIST, LIST)).T for c in range(rows // LIST)], axis=0
     )
+    ids = jnp.where(low_lanes, columns[: rows // 2], columns[rows // 2 :])
+    for_peers(wait_queries)
 
     def one_block(b):
         here = pl.ds(b * span, span)
@@ -242,18 +255,15 @@
     else:
         pl.loop(0, n // span)(one_block)
 
-    @pl.loop(1, n)
-    def _(k):
-        score_copy(k).start()
-
-    keep = pltpu.make_async_copy(best.at[me], arrived.at[me], own_sem.at[0])
+    for_peers(lambda k: score_copy(k).start())
+    keep = pltpu.make_async_copy(best.at[me], arrived.at[me], own_sems.at[0])
     keep.start()
+    for_peers(lambda k: score_copy(k).wait())
     keep.wait()
 
-    @pl.loop(1, n)
-    def _(k):
-        score_copy(k).wait()
-
+
+def finish(arrived, out_ref):
+    n, per_device, _ = arrived.shape
     regs = merge_all(arrived[...].reshape(n * per_device, LIST), per_device)
     table = join(regs).reshape(REGS, SUB, LIST)
     ordered = jnp.concatenate([table[:, s] for s in range(SUB)], axis=0)
@@ -267,30 +277,33 @@
     def local(queries, probes, vectors, list_ids):
         per_device, depth = queries.shape
         rows = vectors.shape[0]
-        return pl.pallas_call(
+        arrived = pl.pallas_call(
             functools.partial(kernel, axes),
-            out_shape=jax.ShapeDtypeStruct((per_device, K), jnp.float32),
-            in_specs=[
-                pl.BlockSpec(memory_space=pltpu.VMEM),
-                pl.BlockSpec(memory_space=pltpu.VMEM),
-                pl.BlockSpec(memory_space=pl.ANY),
-                pl.BlockSpec(memory_space=pltpu.VMEM),
-            ],
-            out_specs=pl.BlockSpec(memory_space=pltpu.VMEM),
+            out_shape=jax.ShapeDtypeStruct((n, per_device, LIST), jnp.float32),
+            in_specs=[pl.BlockSpec(memory_space=pl.ANY)] * 4,
+            out_specs=pl.BlockSpec(memory_space=pl.ANY),
             scratch_shapes=[
+                pltpu.VMEM((per_device, depth), queries.dtype),
+                pltpu.VMEM(probes.shape, probes.dtype),
                 pltpu.VMEM((rows, depth), vectors.dtype),
+                pltpu.VMEM((rows // LIST, LIST), list_ids.dtype),
                 pltpu.VMEM((n, per_device, depth), queries.dtype),
                 pltpu.VMEM((n, per_device, probes.shape[1]), probes.dtype),
                 pltpu.VMEM((n, per_device, LIST), jnp.float32),
-                pltpu.VMEM((n, per_device, LIST), jnp.float32),
-                pltpu.SemaphoreType.DMA,
+                pltpu.SemaphoreType.DMA((4,)),
                 pltpu.SemaphoreType.DMA((2,)),
                 pltpu.SemaphoreType.DMA((2, n)),
                 pltpu.SemaphoreType.DMA((2, n)),
                 pltpu.SemaphoreType.DMA((2, n)),
             ],
             compiler_params=pltpu.CompilerParams(collective_id=0, has_side_effects=True),
-        )(queries, probes, vectors, list_ids[:, None])
+        )(queries, probes, vectors, list_ids.reshape(rows // LIST, LIST))
+        return pl.pallas_call(
+            finish,
+            out_shape=jax.ShapeDtypeStruct((per_device, K), jnp.float32),
+            in_specs=[pl.BlockSpec(memory_space=pltpu.VMEM)],
+            out_specs=pl.BlockSpec(memory_space=pltpu.VMEM),
+        )(arrived)
 
     return jax.shard_map(
         local,

time: 25.4 us -> 21.7 us (0.85)
  local copies, waits for them, and re-layouts: 2.75 us -> 0 us
  Pallas kernels: 22.4 us -> 21.5 us
    pallas_call x1, Pallas kernels: 22.4 us -> 19.4 us  [local(): pl.pallas_call(functools.partial(kernel, axes), out_shape=jax.ShapeDtypeS...]
    pallas_call x0 -> x1, Pallas kernels: none -> 2.04 us  [local(): pl.pallas_call(finish, out_shape=jax.ShapeDtypeStruct((per_device, K), jn...]
    broadcast_in_dim x1 -> x0, local copies, waits for them, and re-layouts: 1.52 us -> none  [local(): list_ids[:, None]]
    unnamed x1 -> x0, local copies, waits for them, and re-layouts: 1.23 us -> none
where the time goes in v2:
time: 21.7 us; the launch traced here: 21.5 us
  Pallas kernels  21.5 us (99%)
    pallas_call x1, Pallas kernels, local(): pl.pallas_call(functools.partial(kernel, axes), out_shape=jax.ShapeDtypeS...  19.4 us
    pallas_call x1, Pallas kernels, local(): pl.pallas_call(finish, out_shape=jax.ShapeDtypeStruct((per_device, K), jn...  2.04 us

profile of v2, /device:TPU:0, one launch (start us, length us, event | category | flops | bytes accessed | tf_op | source)
XLA Modules:
  0.0 21.5 jit_solution(14815972347462531999)
XLA Ops:
  0.0 19.4 %shard_map.46.arrived = f32[32,2,128]{2,1,0:T(2,128)} custom-call(bf16[2,768]{1,0:T(2,128)(2,1)} %q_hbm.1, s32[2,16]{1,0:T(2,128)} %p_hbm.1, bf16[512,768]{1,0:T(8,128)(2,1)} %v_hbm.1, s32[4,128]{1,0:T(4,128)} %bitcast.1), custom_call_target="tpu_custom_call" | custom-call | tf_op jit(solution)/shard_map/pallas_call | solution.py:280
  19.5 2.0 %shard_map.47 = f32[2,100]{1,0:T(2,128)} custom-call(f32[32,2,128]{2,1,0:T(2,128)} %shard_map.46.arrived), custom_call_target="tpu_custom_call" | custom-call | tf_op jit(solution)/shard_map/pallas_call | solution.py:301

commit v3 on v2

--- a/solution.py
+++ b/solution.py
@@ -148,13 +148,14 @@
 
 def kernel(
     axes, q_hbm, p_hbm, v_hbm, id_hbm, arrived,
-    q_ref, p_ref, v_ref, id_ref, all_q, all_p, best, load_sems, own_sems, q_sems, p_sems, s_sems,
+    packed, p_ref, v_ref, id_ref, gathered, best, load_sems, own_sem, q_sems, s_sems,
 ):
     (outer, n_outer), (inner, n_inner) = axes
     n = n_outer * n_inner
     mine = lax.axis_index(outer), lax.axis_index(inner)
     me = mine[0] * n_inner + mine[1]
-    per_device, depth = q_ref.shape
+    per_device, depth = q_hbm.shape
+    n_probes = p_ref.shape[1]
     rows = v_ref.shape[0]
 
     flips = [[(1 - 2 * ((at // 2**i) % 2)) * 2**i for i in range(n_axis.bit_length() - 1)] for at, n_axis in zip(mine, (n_outer, n_inner))]
@@ -171,9 +172,13 @@
         target = flipped(mine[0], flips[0], k // n_inner), flipped(mine[1], flips[1], k % n_inner)
         return target[0] * n_inner + target[1], target
 
+    def reach(k):
+        far, near = divmod(k, n_inner)
+        return near // 2 + near % 2 + (far // 2).bit_count() + 0.25 * (far % 2), k
+
     def for_peers(body):
         if n <= 64:
-            for k in range(n - 1, 0, -1):
+            for k in sorted(range(1, n), key=reach, reverse=True):
                 body(k)
         else:
             pl.loop(1, n)(body)
@@ -182,17 +187,17 @@
     for_peers(lambda k: pl.semaphore_signal(barrier, inc=1, device_id=device(k)[1], device_id_type=MESH))
     loads = [
         pltpu.make_async_copy(src, dst, load_sems.at[i])
-        for i, (src, dst) in enumerate(((q_hbm, q_ref), (p_hbm, p_ref), (id_hbm, id_ref), (v_hbm, v_ref)))
+        for i, (src, dst) in enumerate(((p_hbm, p_ref), (q_hbm, packed.at[:, :depth]), (id_hbm, id_ref), (v_hbm, v_ref)))
     ]
     for copy in loads:
         copy.start()
-    own = [
-        pltpu.make_async_copy(q_ref, all_q.at[me], own_sems.at[0]),
-        pltpu.make_async_copy(p_ref, all_p.at[me], own_sems.at[1]),
-    ]
-    for load, copy in zip(loads[:2], own):
-        load.wait()
-        copy.start()
+    loads[0].wait()
+    digits = jnp.concatenate([p_ref[...] // 256, p_ref[...] % 256], axis=1).astype(jnp.float32)
+    digits = jnp.concatenate([digits, jnp.zeros((per_device, LIST - 2 * n_probes), jnp.float32)], axis=1)
+    packed[:, depth:] = digits.astype(packed.dtype)
+    loads[1].wait()
+    own = pltpu.make_async_copy(packed, gathered.at[me], own_sem)
+    own.start()
     pl.semaphore_wait(barrier, n - 1)
 
     def remote(src, dst, sems, k, target):
@@ -201,24 +206,15 @@
             device_id=target, device_id_type=MESH,
         )
 
-    def query_copies(k):
-        target = device(k)[1]
-        return [remote(q_ref, all_q.at[me], q_sems, k, target), remote(p_ref, all_p.at[me], p_sems, k, target)]
+    def query_copy(k):
+        return remote(packed, gathered.at[me], q_sems, k, device(k)[1])
 
     def score_copy(k):
         other, target = device(k)
         return remote(best.at[other], arrived.at[me], s_sems, k, target)
 
-    def start_queries(k):
-        for copy in query_copies(k):
-            copy.start()
-
-    def wait_queries(k):
-        for copy in query_copies(k):
-            copy.wait()
-
-    for_peers(start_queries)
-    for copy in own + loads[2:]:
+    for_peers(lambda k: query_copy(k).start())
+    for copy in [own] + loads[2:]:
         copy.wait()
 
     lane = lane_index()
@@ -229,22 +225,23 @@
     columns = jnp.concatenate(
         [jnp.broadcast_to(id_ref[c : c + 1], (LIST, LIST)).T for c in range(rows // LIST)], axis=0
     )
-    ids = jnp.where(low_lanes, columns[: rows // 2], columns[rows // 2 :])
-    for_peers(wait_queries)
+    ids = jnp.where(low_lanes, columns[: rows // 2], columns[rows // 2 :]).astype(jnp.float32)
+    for_peers(lambda k: query_copy(k).wait())
 
     def one_block(b):
         here = pl.ds(b * span, span)
-        queries = all_q[here].astype(jnp.float32).reshape(half, depth).astype(jnp.bfloat16)
+        together = gathered[here].astype(jnp.float32).reshape(half, depth + LIST)
+        queries = together[:, :depth].astype(jnp.bfloat16)
         queries = jnp.concatenate([queries, queries], axis=0)
-        probes = all_p[here].reshape(half, all_p.shape[-1])
-        probes = jnp.concatenate([probes, jnp.zeros((half, LIST - probes.shape[1]), jnp.int32)], axis=1)
-        probes = jnp.concatenate([probes, probes], axis=0).T
+        digits = together[:, depth:]
+        digits = jnp.concatenate([digits, digits], axis=0).T
+        probes = digits[:n_probes] * 256.0 + digits[n_probes : 2 * n_probes]
         products = lax.dot_general(
             v_ref[...], queries, (((1,), (1,)), ((), ())), preferred_element_type=jnp.float32
         )
         products = jnp.where(low_lanes, products[: rows // 2], products[rows // 2 :])
         hit = ids == probes[0:1]
-        for p in range(1, all_p.shape[-1]):
+        for p in range(1, n_probes):
             hit = hit | (ids == probes[p : p + 1])
         scores = jnp.where(hit, products, jnp.float32(masked_value))
         kept = join(local_lists(scores, sign))
@@ -256,7 +253,7 @@
         pl.loop(0, n // span)(one_block)
 
     for_peers(lambda k: score_copy(k).start())
-    keep = pltpu.make_async_copy(best.at[me], arrived.at[me], own_sems.at[0])
+    keep = pltpu.make_async_copy(best.at[me], arrived.at[me], own_sem)
     keep.start()
     for_peers(lambda k: score_copy(k).wait())
     keep.wait()
@@ -279,20 +276,18 @@
         rows = vectors.shape[0]
         arrived = pl.pallas_call(
             functools.partial(kernel, axes),
-            out_shape=jax.ShapeDtypeStruct((n, per_device, LIST), jnp.float32),
+            out_shape=pltpu.VMEM((n, per_device, LIST), jnp.float32),
             in_specs=[pl.BlockSpec(memory_space=pl.ANY)] * 4,
-            out_specs=pl.BlockSpec(memory_space=pl.ANY),
+            out_specs=pl.BlockSpec(memory_space=pltpu.VMEM),
             scratch_shapes=[
-                pltpu.VMEM((per_device, depth), queries.dtype),
+                pltpu.VMEM((per_device, depth + LIST), queries.dtype),
                 pltpu.VMEM(probes.shape, probes.dtype),
                 pltpu.VMEM((rows, depth), vectors.dtype),
                 pltpu.VMEM((rows // LIST, LIST), list_ids.dtype),
-                pltpu.VMEM((n, per_device, depth), queries.dtype),
-                pltpu.VMEM((n, per_device, probes.shape[1]), probes.dtype),
+                pltpu.VMEM((n, per_device, depth + LIST), queries.dtype),
                 pltpu.VMEM((n, per_device, LIST), jnp.float32),
                 pltpu.SemaphoreType.DMA((4,)),
-                pltpu.SemaphoreType.DMA((2,)),
-                pltpu.SemaphoreType.DMA((2, n)),
+                pltpu.SemaphoreType.DMA,
                 pltpu.SemaphoreType.DMA((2, n)),
                 pltpu.SemaphoreType.DMA((2, n)),
             ],
@@ -302,6 +297,7 @@
             finish,
             out_shape=jax.ShapeDtypeStruct((per_device, K), jnp.float32),
             in_specs=[pl.BlockSpec(memory_space=pltpu.VMEM)],
+            compiler_params=pltpu.CompilerParams(vmem_limit_bytes=4 << 20),
             out_specs=pl.BlockSpec(memory_space=pltpu.VMEM),
         )(arrived)
 

time: 21.7 us -> 19.6 us (0.903)
  Pallas kernels: 21.5 us -> 19.5 us
    pallas_call x1, Pallas kernels: 19.4 us -> 18.2 us  [local(): pl.pallas_call(functools.partial(kernel, axes), out_shape=pltpu.VMEM((n,...]
    pallas_call x1, Pallas kernels: 2.04 us -> 1.28 us  [local(): pl.pallas_call(finish, out_shape=jax.ShapeDtypeStruct((per_device, K), jn...]
where the time goes in v3:
time: 19.6 us; the launch traced here: 19.5 us
  Pallas kernels  19.5 us (99%)
    pallas_call x1, Pallas kernels, local(): pl.pallas_call(functools.partial(kernel, axes), out_shape=pltpu.VMEM((n,...  18.2 us
    pallas_call x1, Pallas kernels, local(): pl.pallas_call(finish, out_shape=jax.ShapeDtypeStruct((per_device, K), jn...  1.28 us

profile of v3, /device:TPU:0, one launch (start us, length us, event | category | flops | bytes accessed | tf_op | source)
XLA Modules:
  0.0 19.5 jit_solution(4156511454031496426)
XLA Ops:
  0.0 18.2 %shard_map.46.arrived = f32[32,2,128]{2,1,0:T(2,128)S(1)} custom-call(bf16[2,768]{1,0:T(2,128)(2,1)} %q_hbm.1, s32[2,16]{1,0:T(2,128)} %p_hbm.1, bf16[512,768]{1,0:T(8,128)(2,1)} %v_hbm.1, s32[4,128]{1,0:T(4,128)} %bitcast.1), custom_call_target="tpu_custom_call" | custom-call | tf_op jit(solution)/shard_map/pallas_call | solution.py:277
  18.2 1.3 %shard_map.47 = f32[2,100]{1,0:T(2,128)} custom-call(f32[32,2,128]{2,1,0:T(2,128)S(1)} %shard_map.46.arrived), custom_call_target="tpu_custom_call" | custom-call | tf_op jit(solution)/shard_map/pallas_call | solution.py:296

commit v4 on v3

--- a/solution.py
+++ b/solution.py
@@ -226,14 +226,14 @@
         [jnp.broadcast_to(id_ref[c : c + 1], (LIST, LIST)).T for c in range(rows // LIST)], axis=0
     )
     ids = jnp.where(low_lanes, columns[: rows // 2], columns[rows // 2 :]).astype(jnp.float32)
-    for_peers(lambda k: query_copy(k).wait())
+    for_peers(lambda k: query_copy(k).wait_recv())
 
     def one_block(b):
         here = pl.ds(b * span, span)
-        together = gathered[here].astype(jnp.float32).reshape(half, depth + LIST)
-        queries = together[:, :depth].astype(jnp.bfloat16)
+        together = gathered[here].reshape(half, depth + LIST)
+        queries = together[:, :depth]
         queries = jnp.concatenate([queries, queries], axis=0)
-        digits = together[:, depth:]
+        digits = together[:, depth:].astype(jnp.float32)
         digits = jnp.concatenate([digits, digits], axis=0).T
         probes = digits[:n_probes] * 256.0 + digits[n_probes : 2 * n_probes]
         products = lax.dot_general(
@@ -255,8 +255,10 @@
     for_peers(lambda k: score_copy(k).start())
     keep = pltpu.make_async_copy(best.at[me], arrived.at[me], own_sem)
     keep.start()
-    for_peers(lambda k: score_copy(k).wait())
+    for_peers(lambda k: query_copy(k).wait_send())
+    for_peers(lambda k: score_copy(k).wait_send())
     keep.wait()
+    for_peers(lambda k: score_copy(k).wait_recv())
 
 
 def finish(arrived, out_ref):

time: 19.6 us -> 19.5 us (level)
  no operation moved by 1% of the time
where the time goes in v4:
time: 19.5 us; the launch traced here: 19.4 us
  Pallas kernels  19.4 us (99%)
    pallas_call x1, Pallas kernels, local(): pl.pallas_call(functools.partial(kernel, axes), out_shape=pltpu.VMEM((n,...  18.1 us
    pallas_call x1, Pallas kernels, local(): pl.pallas_call(finish, out_shape=jax.ShapeDtypeStruct((per_device, K), jn...  1.28 us

profile of v4, /device:TPU:0, one launch (start us, length us, event | category | flops | bytes accessed | tf_op | source)
XLA Modules:
  0.0 19.4 jit_solution(11336546320906787572)
XLA Ops:
  0.0 18.1 %shard_map.46.arrived = f32[32,2,128]{2,1,0:T(2,128)S(1)} custom-call(bf16[2,768]{1,0:T(2,128)(2,1)} %q_hbm.1, s32[2,16]{1,0:T(2,128)} %p_hbm.1, bf16[512,768]{1,0:T(8,128)(2,1)} %v_hbm.1, s32[4,128]{1,0:T(4,128)} %bitcast.1), custom_call_target="tpu_custom_call" | custom-call | tf_op jit(solution)/shard_map/pallas_call | solution.py:279
  18.1 1.3 %shard_map.47 = f32[2,100]{1,0:T(2,128)} custom-call(f32[32,2,128]{2,1,0:T(2,128)S(1)} %shard_map.46.arrived), custom_call_target="tpu_custom_call" | custom-call | tf_op jit(solution)/shard_map/pallas_call | solution.py:298
